TPU v7x, 32 devices: a whole 2x2x4 slice. The times are simulated.
32 devices in a mesh: member: 2 (over y), tile: 8 (over z, x), sub: 2 (over core).
Axes of the slice: x: 2, y: 2, z: 4, core: 2. Of those that a mesh axis runs over, the one named last changes fastest.
Arguments:
- atm_state: bfloat16 [8, 32768], P(None, ('member', 'tile')), parts along dimension 1, may hold values from -6 to 6
- ocn_state: bfloat16 [4, 32768], P(None, ('member', 'tile', 'sub')), parts along dimension 1, may hold values from -6 to 6
- need_atm: int32 [128], P(('tile', 'sub')), may hold values from 0 to 127, as said below
- xb_need: int32 [128], P(('tile', 'sub')), may hold values from 0 to 15
- xb_ocn: int32 [128], P(('tile', 'sub')), may hold values from 0 to 15
- xb_count: int32 [16], P(('tile', 'sub')), may hold values from 1 to 8, as said below
- sea_mask: int32 [16384], P(('tile', 'sub')), may hold values 0 or 1
- cell_area: float32 [16384], P(('tile', 'sub')), may hold values from 0.5 to 2
- w_atm: bfloat16 [128, 128, 128], P(('tile', 'sub')), may hold values from 0.0099487305 to 1
- w_ocn: bfloat16 [128, 128, 128], P(('tile', 'sub')), may hold values from 0.0099487305 to 1
Outputs:
- atm_flux: float32 [4, 32768], P(None, ('member', 'tile')), parts along dimension 1
- ocn_flux: float32 [4, 32768], P(None, ('member', 'tile', 'sub')), parts along dimension 1
There are 2 independent parts, one for each index of `member`. A program takes and returns all parts, laid end to end along the dimension named above; an argument that names none is the same for every part. Nothing has to cross between parts.
Inputs may be any that keep to these rules, and one draw needn't show every extreme that they name: `need_atm`: an atmosphere block n lies on tile n // 16. A tile's list is the entries of its devices in device order; for tile t its entries 2 i and 2 i + 1 lie on tile (t + i - 8 // 2 + 1) mod 8 for i < 7, and on tile (t + 4) mod 8 for i = 7; all entries of one tile's list are distinct. `xb_need`: index into the list of the block's tile. `xb_ocn`: index among the ocean blocks of the block's tile, in device order. `xb_count`: some device has all 8 blocks live.
All inputs are finite; a program needn't handle non-finite values. No bound on the sum of `sea_mask` on one device may be relied on, other than what follows from the above.
Results may differ from a plain program's by a relative error of at most 0.0003.
Values may be sent and summed in bfloat16 or wider, within the bound.
A program may use at most 64 MiB of HBM per device.

v0:
```python
import jax
import jax.numpy as jnp
from jax import lax
from jax.sharding import PartitionSpec as P

CAP = 2


def bulk_fluxes(upper_domain_vector, marine_regrid_transfer):
    (
        lowest_level_warmth,
        vapour_mixing_ratio,
        eastward_wind,
        northward_wind,
        ground_level_pressure,
        solar_radiation,
        infrared_radiation,
        rainfall_rate,
    ) = [upper_domain_vector[:, grid_box_number] for grid_box_number in range(8)]
    skin_warmth_kelvin, eastward_current, northward_current, marine_climate_coupler = [
        marine_regrid_transfer[:, grid_box_number] for grid_box_number in range(4)
    ]
    du = eastward_wind - eastward_current
    dv = northward_wind - northward_current
    speed = jnp.sqrt(du * du + dv * dv + 1.0)
    momentum_transfer_factor = (0.3 + 0.1 * jnp.tanh(ground_level_pressure)) * speed
    conductive_energy_loss = momentum_transfer_factor * (skin_warmth_kelvin - lowest_level_warmth)
    evaporative_energy_loss = momentum_transfer_factor * (
        0.5 * skin_warmth_kelvin - vapour_mixing_ratio
    )
    taux = momentum_transfer_factor * du
    tauy = momentum_transfer_factor * dv
    reflected_fraction = 0.06 + 0.1 * jax.nn.sigmoid(marine_climate_coupler)
    thermal_energy_transfer = (
        (1.0 - reflected_fraction) * solar_radiation
        + infrared_radiation
        - 0.2 * skin_warmth_kelvin
        - conductive_energy_loss
        - evaporative_energy_loss
    )
    fresh = rainfall_rate - 0.5 * evaporative_energy_loss
    return (
        jnp.stack([conductive_energy_loss, evaporative_energy_loss, taux, tauy], 1),
        jnp.stack([thermal_energy_transfer, taux, tauy, fresh], 1),
    )


def per_device(
    atm_state, ocn_state, need_atm, xb_need, xb_ocn, xb_count, sea_mask, cell_area, w_atm, w_ocn
):
    highest = lax.Precision.HIGHEST
    ntile = lax.axis_size("tile")
    fields_a = atm_state.shape[0]
    fields_o = ocn_state.shape[0]
    blk = w_atm.shape[1]
    nblocks = w_atm.shape[0]
    owned_blocks = atm_state.shape[1] // blk
    table = jnp.transpose(atm_state.reshape(fields_a, owned_blocks, blk), (1, 0, 2))
    depth = CAP
    wanted = lax.all_gather(need_atm, "sub", axis=0, tiled=True)
    owner = wanted // owned_blocks
    local = wanted % owned_blocks
    order = jnp.arange(wanted.shape[0], dtype=jnp.int32)
    earlier = (owner[:, None] == owner[None, :]) & (order[None, :] < order[:, None])
    rank = jnp.sum(earlier.astype(jnp.int32), axis=1)
    slot = owner * depth + rank
    placed = (slot[:, None] == jnp.arange(ntile * depth, dtype=jnp.int32)[None, :]).astype(
        jnp.int32
    )
    asked_all = (jnp.sum(placed * (local[:, None] + 1), axis=0) - 1).reshape(ntile, depth)
    received = lax.all_to_all(asked_all, "tile", split_axis=0, concat_axis=0, tiled=True)
    flat = received.reshape(-1)
    picked = table[jnp.maximum(flat, 0)]
    picked = jnp.where((flat >= 0)[:, None, None], picked, jnp.zeros_like(picked))
    answer = lax.all_to_all(
        picked.reshape(ntile, depth, fields_a, blk), "tile", split_axis=0, concat_axis=0, tiled=True
    )
    fetched = answer.reshape(ntile * depth, fields_a, blk)[slot]
    ocean_all = lax.all_gather(ocn_state, "sub", axis=1, tiled=True)
    ocean_table = jnp.transpose(ocean_all.reshape(fields_o, -1, blk), (1, 0, 2))
    upper_domain_vector = jnp.einsum(
        "bfj,bxj->bfx", fetched[xb_need], w_atm, preferred_element_type=jnp.float32
    )
    upper_domain_vector = (
        upper_domain_vector / jnp.sum(w_atm, axis=2, dtype=jnp.float32)[:, None, :]
    )
    marine_regrid_transfer = jnp.einsum(
        "bfj,bxj->bfx", ocean_table[xb_ocn], w_ocn, preferred_element_type=jnp.float32
    )
    marine_regrid_transfer = (
        marine_regrid_transfer / jnp.sum(w_ocn, axis=2, dtype=jnp.float32)[:, None, :]
    )
    to_atm, to_ocn = bulk_fluxes(upper_domain_vector, marine_regrid_transfer)
    live = (jnp.arange(nblocks, dtype=jnp.int32) < xb_count[0]).astype(jnp.float32)[:, None]
    weighted = cell_area.reshape(nblocks, blk) * live
    wet = weighted * sea_mask.reshape(nblocks, blk).astype(jnp.float32)
    atm_terms = jnp.concatenate([to_atm * wet[:, None, :], weighted[:, None, :]], 1)
    ocn_terms = jnp.concatenate([to_ocn * wet[:, None, :], wet[:, None, :]], 1)
    atm_cells = jnp.einsum(
        "bgx,bxj->bgj", atm_terms, w_atm, precision=highest, preferred_element_type=jnp.float32
    )
    ocn_cells = jnp.einsum(
        "bgx,bxj->bgj", ocn_terms, w_ocn, precision=highest, preferred_element_type=jnp.float32
    )
    list_len = fetched.shape[0]
    select_a = (xb_need[:, None] == jnp.arange(list_len, dtype=jnp.int32)[None, :]).astype(
        jnp.float32
    )
    list_terms = jnp.einsum("bn,bgj->ngj", select_a, atm_cells, precision=highest)
    outgoing = (
        jnp.zeros((ntile * depth,) + list_terms.shape[1:], jnp.float32).at[slot].set(list_terms)
    )
    incoming = lax.all_to_all(
        outgoing.reshape((ntile, depth) + list_terms.shape[1:]),
        "tile",
        split_axis=0,
        concat_axis=0,
        tiled=True,
    )
    incoming = incoming.reshape((ntile * depth,) + list_terms.shape[1:])
    landing = (flat[:, None] == jnp.arange(owned_blocks, dtype=jnp.int32)[None, :]).astype(
        jnp.float32
    )
    owned = jnp.einsum("sa,sgc->agc", landing, incoming, precision=highest)
    totals = lax.psum(owned, "sub")
    nflux = totals.shape[1] - 1
    atm_flux = totals[:, :nflux] / jnp.maximum(totals[:, nflux:], 1.0)
    atm_flux = jnp.transpose(atm_flux, (1, 0, 2)).reshape(nflux, owned_blocks * blk)
    ocean_len = ocean_table.shape[0]
    select_o = (xb_ocn[:, None] == jnp.arange(ocean_len, dtype=jnp.int32)[None, :]).astype(
        jnp.float32
    )
    ocean_terms = jnp.einsum("bn,bgj->ngj", select_o, ocn_cells, precision=highest)
    ocean_mine = lax.psum_scatter(ocean_terms, "sub", scatter_dimension=0, tiled=True)
    ocn_flux = ocean_mine[:, :nflux] / jnp.maximum(ocean_mine[:, nflux:], 1.0)
    ocn_flux = jnp.transpose(ocn_flux, (1, 0, 2)).reshape(nflux, -1)
    return (atm_flux, ocn_flux)


def solution(mesh):
    placed = (
        P(None, ("member", "tile")),
        P(None, ("member", "tile", "sub")),
        P(("tile", "sub")),
        P(("tile", "sub")),
        P(("tile", "sub")),
        P(("tile", "sub")),
        P(("tile", "sub")),
        P(("tile", "sub")),
        P(("tile", "sub"), None, None),
        P(("tile", "sub"), None, None),
    )
    return jax.shard_map(
        per_device,
        mesh=mesh,
        in_specs=placed,
        out_specs=(P(None, ("member", "tile")), P(None, ("member", "tile", "sub"))),
        check_vma=False,
    )
```

profile of v0, /device:TPU:0, one launch (start us, length us, event | category | flops | bytes accessed | tf_op | source)
XLA Modules:
  0.0 72.2 jit_solution(7905049220486723166)
XLA Ops:
  7.2 0.0 copy-start
  7.2 0.0 copy-start.6
  7.2 0.0 copy-start.2
  7.2 0.6 copy-done.6
  7.8 0.6 dynamic-slice
  9.1 0.9 %dynamic-update-slice = s32[16]{0:T(128)S(1)} dynamic-update-slice(s32[16]{0:T(128)S(1)} %broadcast.152, s32[8]{0:T(128)} %param.12, u32[]{:T(128)} %bitcast) | dynamic-update-slice | bytes 68
  9.9 2.0 %all-reduce = s32[16]{0:T(128)S(1)} all-reduce(s32[16]{0:T(128)S(1)} %dynamic-update-slice), channel_id=1, replica_groups=mesh['member'=2,'tile'=8,'sub'=2] {'sub'}, use_global_device_ids=true, to_apply=%add | all-reduce | flops 16 | bytes 128
  11.9 0.2 convert_reduce_fusion.2
  12.1 0.1 select_reduce_fusion
  12.2 0.7 sub.60
  12.9 7.1 %all-to-all-start = ((s32[8,1,2]{2,1,0:T(1,128)}), s32[8,1,2]{2,1,0:T(1,128)S(1)}, u32[]{:S(2)}, u32[]{:S(2)}) async-start(s32[8,1,2]{2,1,0:T(1,128)} %bitcast.1), calls=%async_computation | async-start | bytes 8192 | tf_op jit(solution)/shard_map/all_to_all | solution.py:71
  20.7 0.8 %bitcast_multiply_fusion.2 = f32[8,128]{1,0:T(8,128)S(1)} fusion(f32[1024]{0:T(1024)} %param.17, s32[1024]{0:T(1024)} %param.16, f32[8]{0:T(128)S(1)} %compare_convert_fusion), kind=kLoop, calls=%fused_computation.69 | loop fusion | flops 3072 | bytes 12320 | tf_op jit(solution)/shard_map/mul | solution.py:96
  21.5 0.8 %bitcast_multiply_fusion = (f32[8,1,128]{2,0,1:T(8,128)S(1)}, f32[8,1,128]{2,0,1:T(8,128)S(1)}) fusion(s32[1024]{0:T(1024)} %param.16, f32[8]{0:T(128)S(1)} %compare_convert_fusion, f32[1024]{0:T(1024)} %param.17), kind=kLoop, calls=%fused_computation.67 | loop fusion | flops 3072 | bytes 16416 | tf_op jit(solution)/shard_map/mul | solution.py:96
  22.2 0.7 compare_select_fusion.1
  22.9 0.7 compare_select_fusion
  23.6 1.1 %convert_reduce_fusion.1 = f32[8,128]{1,0:T(8,128)S(1)} fusion(bf16[8,128,128]{2,1,0:T(8,128)(2,1)} %param.18), kind=kLoop, calls=%fused_computation.6 | loop fusion | flops 261120 | bytes 266240 | tf_op jit(solution)/shard_map/reduce_sum | solution.py:85
  24.7 0.0 copy-done.2
  24.7 0.0 copy-start.3
  24.7 0.1 convert_reduce_fusion
  24.8 0.5 copy-done.3
  25.4 1.8 %all_gather.7 = bf16[4,2048]{1,0:T(4,128)(2,1)S(1)} all-gather(bf16[4,1024]{1,0:T(4,128)(2,1)S(1)} %copy-done.3), channel_id=1, replica_groups=mesh['member'=2,'tile'=8,'sub'=2] {'sub'}, dimensions={1}, use_global_device_ids=true | all-gather | bytes 24576 | tf_op jit(solution)/shard_map/all_gather | solution.py:79
  27.2 0.6 gather_fusion.3
  27.7 0.2 fusion.45
  28.0 0.0 copy-start.1
  28.0 0.0 all-to-all-done
  28.0 0.1 copy.39
  28.1 0.1 copy.40
  28.2 0.5 broadcast.203
  28.8 0.7 fusion.40
  29.4 0.1 reshape.170
  29.5 0.0 copy-done
  29.5 0.6 gather_fusion
  30.1 0.7 broadcast_select_fusion
  30.8 6.0 %all-to-all-start.1 = ((bf16[8,2,8,128]{3,2,1,0:T(8,128)(2,1)}), bf16[8,2,8,128]{3,2,1,0:T(8,128)(2,1)S(1)}, u32[]{:S(2)}, u32[]{:S(2)}) async-start(bf16[8,2,8,128]{3,2,1,0:T(8,128)(2,1)} %broadcast_select_fusion), calls=%async_computation.1 | async-start | bytes 65536 | tf_op jit(solution)/shard_map/all_to_all | solution.py:75
  36.8 0.1 eq.35
  36.9 6.6 %all-to-all-done.1 = bf16[8,2,8,128]{3,2,1,0:T(8,128)(2,1)S(1)} async-done(((bf16[8,2,8,128]{3,2,1,0:T(8,128)(2,1)}), bf16[8,2,8,128]{3,2,1,0:T(8,128)(2,1)S(1)}, u32[]{:S(2)}, u32[]{:S(2)}) %all-to-all-start.1) | async-done | bytes 32800 | tf_op jit(solution)/shard_map/all_to_all | solution.py:75
  43.5 0.6 gather_fusion.1
  44.1 0.6 gather_fusion.2
  44.6 0.0 copy-done.1
  44.6 0.2 fusion.44
  45.0 0.0 copy-start.4
  45.0 0.3 fusion.3
  45.3 0.3 copy-done.4
  45.6 0.3 fusion.7
  45.9 0.3 fusion.1
  46.3 1.0 %scatter_fusion = f32[16,5,128]{2,1,0:T(8,128)S(1)} fusion(f32[16,5,128]{2,1,0:T(8,128)S(1)} %broadcast_in_dim.18, s32[16]{0:T(128)S(1)} %get-tuple-element.10, f32[16,5,128]{2,1,0:T(8,128)S(1)} %copy.45), kind=kCustom, calls=%fused_computation.4 | custom fusion | bytes 122944 | tf_op jit(solution)/shard_map/scatter | solution.py:111
  47.3 0.6 copy.46
  47.9 0.0 copy-start.5
  47.9 3.5 %all-to-all-start.2 = ((f32[8,2,5,128]{3,1,2,0:T(2,128)}), f32[8,2,5,128]{3,1,2,0:T(2,128)S(1)}, u32[]{:S(2)}, u32[]{:S(2)}) async-start(f32[8,2,5,128]{3,1,2,0:T(2,128)} %copy.46), calls=%async_computation.2 | async-start | bytes 81920 | tf_op jit(solution)/shard_map/all_to_all | solution.py:113
  51.4 0.0 reduce-scatter.2.cloned.1.call-start
  51.5 0.0 copy-done.5
  51.5 0.9 %fusion.5 = f32[16,5,128]{2,0,1:T(8,128)} fusion(f32[8,5,128]{2,1,0:T(8,128)S(1)} %fusion.1, s32[8]{0:T(128)S(1)} %copy-done.5), kind=kOutput, calls=%fused_computation.18 | convolution fusion | flops 983168 | bytes 61472 | tf_op jit(solution)/shard_map/bn,bgj->ngj/dot_general | solution.py:133
  52.4 0.0 reduce-scatter.2.cloned.1.call-update
  52.4 5.7 %all-to-all-done.2 = f32[8,2,5,128]{3,1,2,0:T(2,128)S(1)} async-done(((f32[8,2,5,128]{3,1,2,0:T(2,128)}), f32[8,2,5,128]{3,1,2,0:T(2,128)S(1)}, u32[]{:S(2)}, u32[]{:S(2)}) %all-to-all-start.2) | async-done | bytes 40992 | tf_op jit(solution)/shard_map/all_to_all | solution.py:113
  58.1 0.1 fusion.13
  58.3 3.5 %psum.7 = f32[16,5,128]{2,0,1:T(8,128)S(1)} all-reduce(f32[16,5,128]{2,0,1:T(8,128)S(1)} %fusion.13), channel_id=1, replica_groups=mesh['member'=2,'tile'=8,'sub'=2] {'sub'}, use_global_device_ids=true, to_apply=%region_5.6 | all-reduce | flops 10240 | bytes 81920 | tf_op jit(solution)/shard_map/psum | solution.py:125
  61.8 0.6 copy.64
  62.4 0.9 %reduce-scatter.2.cloned.1.call-done = f32[8,5,128]{2,0,1:T(8,128)} async-done(((f32[16,5,128]{2,0,1:T(8,128)}), f32[8,5,128]{2,0,1:T(8,128)}) %reduce-scatter.2.cloned.1.call-update) | async-done | bytes 20496 | tf_op jit(solution)/shard_map/reduce_scatter | solution.py:134
  63.3 0.7 fusion.15
  64.0 0.7 fusion.9
  64.7 0.6 copy.65
  (21 shorter events, 0.2 us)
Async XLA Ops:
  7.2 22.4 %copy-start = (bf16[8,2048]{1,0:T(8,128)(2,1)S(1)}, bf16[8,2048]{1,0:T(8,128)(2,1)}, u32[]{:S(2)}) copy-start(bf16[8,2048]{1,0:T(8,128)(2,1)} %param.10) | copy-start | bytes 98308
  7.2 0.7 copy-start.6
  7.2 17.5 %copy-start.2 = (bf16[8,128,128]{2,1,0:T(8,128)(2,1)S(1)}, bf16[8,128,128]{2,1,0:T(8,128)(2,1)}, u32[]{:S(2)}) copy-start(bf16[8,128,128]{2,1,0:T(8,128)(2,1)} %param.19) | copy-start | bytes 786436
  12.9 15.1 %all-to-all-start = ((s32[8,1,2]{2,1,0:T(1,128)}), s32[8,1,2]{2,1,0:T(1,128)S(1)}, u32[]{:S(2)}, u32[]{:S(2)}) async-start(s32[8,1,2]{2,1,0:T(1,128)} %bitcast.1), calls=%async_computation | async-start | bytes 8192 | tf_op jit(solution)/shard_map/all_to_all | solution.py:71
  24.7 0.7 copy-start.3
  28.0 16.7 %copy-start.1 = (bf16[8,128,128]{2,1,0:T(8,128)(2,1)S(1)}, bf16[8,128,128]{2,1,0:T(8,128)(2,1)}, u32[]{:S(2)}) copy-start(bf16[8,128,128]{2,1,0:T(8,128)(2,1)} %param.18) | copy-start | bytes 786436
  30.8 12.7 %all-to-all-start.1 = ((bf16[8,2,8,128]{3,2,1,0:T(8,128)(2,1)}), bf16[8,2,8,128]{3,2,1,0:T(8,128)(2,1)S(1)}, u32[]{:S(2)}, u32[]{:S(2)}) async-start(bf16[8,2,8,128]{3,2,1,0:T(8,128)(2,1)} %broadcast_select_fusion), calls=%async_computation.1 | async-start | bytes 65536 | tf_op jit(solution)/shard_map/all_to_all | solution.py:75
  45.0 0.7 copy-start.4
  47.9 3.5 %copy-start.5 = (s32[8]{0:T(128)S(1)}, s32[8]{0:T(128)}, u32[]{:S(2)}) copy-start(s32[8]{0:T(128)} %param.14) | copy-start | bytes 100
  47.9 10.2 %all-to-all-start.2 = ((f32[8,2,5,128]{3,1,2,0:T(2,128)}), f32[8,2,5,128]{3,1,2,0:T(2,128)S(1)}, u32[]{:S(2)}, u32[]{:S(2)}) async-start(f32[8,2,5,128]{3,1,2,0:T(2,128)} %copy.46), calls=%async_computation.2 | async-start | bytes 81920 | tf_op jit(solution)/shard_map/all_to_all | solution.py:113
  51.4 11.9 %reduce-scatter.2.cloned.1.call-start = ((), (), s32[]{:S(2)}) async-start(), calls=%async_computation.4 | async-start | bytes 61440 | tf_op jit(solution)/shard_map/reduce_scatter | solution.py:134
Sparse Core Ops, SparseCore 0:
  54.4 8.8 reduce-scatter.1
where the time goes:
time: 72.9 us; the launch traced here: 72.2 us
  starting transfers between devices  16.6 us (23%)
  between operations  15.6 us (21%)
  waiting for transfers between devices  13.3 us (18%)
  local copies, waits for them, and re-layouts  9.76 us (13%)
  other arithmetic  7.32 us (10%)
  blocking collectives  7.24 us (10%)
  matrix products  2.39 us (3%)
    all_to_all x1, starting transfers between devices, per_device(): lax.all_to_all(asked_all, 'tile', split_axis=0, concat_axis=0, tiled=True)  7.13 us
    all_to_all x1, waiting for transfers between devices, per_device(): lax.all_to_all(picked.reshape(ntile, depth, fields_a, blk), 'tile', split...  6.6 us
    all_to_all x1, starting transfers between devices, per_device(): lax.all_to_all(picked.reshape(ntile, depth, fields_a, blk), 'tile', split...  6 us
    all_to_all x1, waiting for transfers between devices, per_device(): lax.all_to_all(outgoing.reshape((ntile, depth) + list_terms.shape[1:]), '...  5.71 us
    unnamed x19, local copies, waits for them, and re-layouts  4.23 us
    psum x1, blocking collectives, per_device(): totals = lax.psum(owned, 'sub')  3.48 us
    all_to_all x1, starting transfers between devices, per_device(): lax.all_to_all(outgoing.reshape((ntile, depth) + list_terms.shape[1:]), '...  3.47 us
    unnamed x1, blocking collectives  1.96 us
  transfers between devices with their start and end apart: 4, of which 3 were waited for; matrix products, arithmetic and copies ran while one was open for 9% of the time, Pallas kernels for 0%

commit v1 on v0

v1 whole, which is shorter than its diff:
```python
import functools

import jax
import jax.numpy as jnp
from jax import lax
from jax.experimental import pallas as pl
from jax.experimental.pallas import tpu as pltpu
from jax.sharding import PartitionSpec as P

MESH = pl.DeviceIdType.MESH
ROWS = 8
PAIR = 2
F32 = jnp.float32
BF16 = jnp.bfloat16
TRANSPOSED = (((1,), (1,)), ((), ()))


def split(value):
    high = value.astype(BF16)
    low = (value - high.astype(F32)).astype(BF16)
    return high, low


def kernel(
    ntile, nsub, blk,
    state_hbm, ocean_hbm, need_hbm, xbn_hbm, xbo_hbm, count_hbm, sea_hbm, area_hbm, wa_hbm, wo_hbm,
    atm_out, ocn_out,
    state, octab, need, xbn, xbo, count, sea, area, wa, wo,
    table, picked, rows_send, rows_recv, sums_send, sums_recv, oc_send, oc_recv, atm_v, ocn_v,
    load_sem, block_sem, push_ssem, push_rsem, row_ssem, row_rsem, oc_ssem, oc_rsem,
    pick_ssem, pick_rsem, sum_ssem, sum_rsem, ob_ssem, ob_rsem, out_sem,
):
    me = lax.axis_index("tile")
    core = lax.axis_index("sub")
    other = 1 - core
    nb = wa.shape[0]
    mine = need.shape[0]
    half = mine // PAIR
    owners = half * nsub
    entries = mine * nsub
    owned = state.shape[0]
    obl = octab.shape[1]
    nflux = atm_v.shape[0]

    def offset(i):
        return ntile // 2 if i == owners - 1 else i - owners // 2 + 1

    def tile_at(delta):
        return lax.rem(me + delta + ntile, ntile)

    zero_i = [i for i in range(owners) if offset(i) == 0][0]

    local = [
        pltpu.make_async_copy(src, dst, load_sem.at[k])
        for k, (src, dst) in enumerate(
            [
                (need_hbm, need),
                (wo_hbm, wo),
                (wa_hbm, wa),
                (xbo_hbm, xbo),
                (xbn_hbm, xbn),
                (count_hbm, count),
                (sea_hbm, sea),
                (area_hbm, area),
            ]
        )
    ]
    blocks = [
        pltpu.make_async_copy(
            state_hbm.at[:, pl.ds(n * blk, blk)], state.at[n], block_sem.at[n]
        )
        for n in range(owned)
    ] + [
        pltpu.make_async_copy(
            ocean_hbm.at[:, pl.ds(n * blk, blk)], octab.at[core, n], block_sem.at[owned + n]
        )
        for n in range(obl)
    ]
    for copy in blocks + local:
        copy.start()

    barrier = pltpu.get_barrier_semaphore()
    for i in range(owners):
        for c in range(nsub):
            if i == zero_i:
                continue
            pl.semaphore_signal(
                barrier, inc=1, device_id={"tile": tile_at(offset(i)), "sub": c}, device_id_type=MESH
            )
    pl.semaphore_signal(barrier, inc=1, device_id={"tile": me, "sub": other}, device_id_type=MESH)

    local[0].wait()
    lane = lax.broadcasted_iota(jnp.int32, (1, blk), 1)
    odd = lax.rem(lane // ROWS, PAIR)
    for k in range(half):
        first = lax.rem(need[PAIR * k], owned)
        second = lax.rem(need[PAIR * k + 1], owned)
        rows_send[k] = jnp.where(odd == 0, first, second)
    for copy in blocks:
        copy.wait()
    pl.semaphore_wait(barrier, owners * nsub - 1)

    def delta_of(k):
        out = jnp.int32(0)
        for c in range(nsub):
            out = jnp.where(core == c, jnp.int32(offset(c * half + k)), out)
        return out

    deltas = [delta_of(k) for k in range(half)]
    pushes = [
        pltpu.make_async_remote_copy(
            src_ref=state,
            dst_ref=table.at[k],
            send_sem=push_ssem.at[k],
            recv_sem=push_rsem.at[k],
            device_id={"tile": tile_at(-deltas[k]), "sub": core},
            device_id_type=MESH,
        )
        for k in range(half)
    ]
    keep = pltpu.make_async_copy(state, table.at[zero_i % half], out_sem.at[0])
    zero_core = zero_i // half
    order = sorted(range(half), key=lambda k: -abs(offset(k)))
    for k in order:
        if k == zero_i % half:
            @pl.when(core == zero_core)
            def _():
                keep.start()

            @pl.when(core != zero_core)
            def _(k=k):
                pushes[k].start()
        else:
            pushes[k].start()
    oc_copy = pltpu.make_async_remote_copy(
        src_ref=octab.at[core],
        dst_ref=octab.at[core],
        send_sem=oc_ssem,
        recv_sem=oc_rsem,
        device_id={"tile": me, "sub": other},
        device_id_type=MESH,
    )
    oc_copy.start()

    row_copies = []
    for k in range(half):
        slot = core * half + k
        for c in range(nsub):
            row_copies.append(
                pltpu.make_async_remote_copy(
                    src_ref=rows_send.at[k],
                    dst_ref=rows_recv.at[slot],
                    send_sem=row_ssem.at[k * nsub + c],
                    recv_sem=row_rsem.at[slot],
                    device_id={"tile": tile_at(deltas[k]), "sub": c},
                    device_id_type=MESH,
                )
            )
            copy = row_copies[-1]
            if k == zero_i % half:
                here = jnp.logical_and(core == zero_core, core == c)

                @pl.when(here)
                def _(k=k):
                    rows_recv[zero_i] = rows_send[k]

                @pl.when(jnp.logical_not(here))
                def _(copy=copy):
                    copy.start()
            else:
                copy.start()

    ones = jnp.ones((ROWS, blk), BF16)
    local[1].wait()
    local[3].wait()
    oc_copy.wait_recv()
    oxs = []
    for b in range(nb):
        m = xbo[b]
        cells = octab[lax.div(m, obl), lax.rem(m, obl)]
        w = wo[b]
        top = lax.dot_general(cells, w, TRANSPOSED, preferred_element_type=F32)
        den = lax.dot_general(ones, w, TRANSPOSED, preferred_element_type=F32)
        oxs.append(top / den[: top.shape[0]])
    ox = jnp.concatenate(oxs, axis=1)
    sst, uo, vo, oa = [ox[f : f + 1] for f in range(4)]
    albedo = 0.06 + 0.05 * (1.0 + jnp.tanh(0.5 * oa))
    local[2].wait()
    dens = jnp.concatenate(
        [lax.dot_general(ones, wa[b], TRANSPOSED, preferred_element_type=F32) for b in range(nb)],
        axis=1,
    )
    rden = 1.0 / dens
    for k in (4, 5, 6, 7):
        local[k].wait()
    cell = lax.broadcasted_iota(jnp.int32, (1, nb * blk), 1)
    weighted = jnp.where(cell < count[0] * blk, area[...], 0.0)
    wet = weighted * sea[...].astype(F32)

    for k in range(half):
        if k == zero_i % half:
            @pl.when(core == zero_core)
            def _():
                keep.wait()

            @pl.when(core != zero_core)
            def _(k=k):
                pushes[k].wait_recv()
        else:
            pushes[k].wait_recv()
    for e in range(mine):
        picked[core * mine + e] = table[e // PAIR, lax.rem(need[e], owned)]
    part = picked.at[pl.ds(core * mine, mine)]
    pick_copy = pltpu.make_async_remote_copy(
        src_ref=part,
        dst_ref=part,
        send_sem=pick_ssem,
        recv_sem=pick_rsem,
        device_id={"tile": me, "sub": other},
        device_id_type=MESH,
    )
    pick_copy.start()
    pick_copy.wait_recv()
    ax = jnp.concatenate(
        [
            lax.dot_general(picked[xbn[b]], wa[b], TRANSPOSED, preferred_element_type=F32)
            for b in range(nb)
        ],
        axis=1,
    )
    ax = ax * rden
    ta, qa, ua, va, ps, sw, lw, pr = [ax[f : f + 1] for f in range(8)]

    du = ua - uo
    dv = va - vo
    speed = jnp.sqrt(du * du + dv * dv + 1.0)
    cd = (0.3 + 0.1 * jnp.tanh(ps)) * speed
    sens = cd * (sst - ta)
    lat = cd * (0.5 * sst - qa)
    taux = cd * du
    tauy = cd * dv
    pad = jnp.zeros((ROWS - 5, nb * blk), F32)
    atm_terms = jnp.concatenate([sens * wet, lat * wet, taux * wet, tauy * wet, weighted, pad], 0)
    both = jnp.concatenate(split(atm_terms), axis=0)

    def spread(both, w, index, number):
        totals = [None] * number
        for b in range(nb):
            prod = jnp.dot(both[:, b * blk : (b + 1) * blk], w[b], preferred_element_type=F32)
            prod = prod[:ROWS] + prod[ROWS:]
            at = jnp.full((ROWS, blk), index[b], jnp.int32)
            for n in range(number):
                term = jnp.where(at == n, prod, 0.0)
                totals[n] = term if totals[n] is None else totals[n] + term
        return totals

    totals = spread(both, wa, xbn, entries)
    for n in range(entries):
        sums_send[n // PAIR, (n % PAIR) * ROWS : (n % PAIR + 1) * ROWS] = totals[n]
    sum_copies = {}
    for i in sorted(range(owners), key=lambda i: -abs(offset(i))):
        for c in range(nsub):
            if i == zero_i:
                continue
            sum_copies[i, c] = pltpu.make_async_remote_copy(
                src_ref=sums_send.at[i],
                dst_ref=sums_recv.at[core, i],
                send_sem=sum_ssem.at[i, c],
                recv_sem=sum_rsem.at[core, i],
                device_id={"tile": tile_at(offset(i)), "sub": c},
                device_id_type=MESH,
            )
            sum_copies[i, c].start()
    self_copy = pltpu.make_async_remote_copy(
        src_ref=sums_send.at[zero_i],
        dst_ref=sums_recv.at[core, zero_i],
        send_sem=sum_ssem.at[zero_i, 0],
        recv_sem=sum_rsem.at[core, zero_i],
        device_id={"tile": me, "sub": other},
        device_id_type=MESH,
    )
    self_copy.start()
    for e in range(PAIR):
        sums_recv[core, zero_i, e * ROWS : (e + 1) * ROWS] = totals[PAIR * zero_i + e]

    heat = (1.0 - albedo) * sw + lw - 0.2 * sst - sens - lat
    fresh = pr - 0.5 * lat
    ocn_terms = jnp.concatenate([heat * wet, taux * wet, tauy * wet, fresh * wet, wet, pad], 0)
    ototals = spread(jnp.concatenate(split(ocn_terms), axis=0), wo, xbo, obl * nsub)
    own = []
    for m in range(obl):
        low, high = ototals[m], ototals[obl + m]
        oc_send[m] = jnp.where(core == 0, high, low)
        own.append(jnp.where(core == 0, low, high))
    ob_copy = pltpu.make_async_remote_copy(
        src_ref=oc_send,
        dst_ref=oc_recv,
        send_sem=ob_ssem,
        recv_sem=ob_rsem,
        device_id={"tile": me, "sub": other},
        device_id_type=MESH,
    )
    ob_copy.start()

    def recv_desc(src, dst, ssem, rsem):
        return pltpu.make_async_remote_copy(
            src_ref=src, dst_ref=dst, send_sem=ssem, recv_sem=rsem,
            device_id={"tile": me, "sub": other}, device_id_type=MESH,
        )

    for i in range(owners):
        desc = recv_desc(rows_send.at[0], rows_recv.at[i], row_ssem.at[0], row_rsem.at[i])
        if i == zero_i:
            @pl.when(core != zero_core)
            def _(desc=desc):
                desc.wait_recv()
        else:
            desc.wait_recv()
    width = owners * PAIR * ROWS
    places = jnp.concatenate([rows_recv[i] for i in range(owners)], axis=0)
    slot_of = lax.broadcasted_iota(jnp.int32, (owners, width), 1) // (PAIR * ROWS)
    mask = slot_of == lax.broadcasted_iota(jnp.int32, (owners, width), 0)
    place = jnp.sum(jnp.where(mask, places, 0), axis=0, keepdims=True)
    down = lax.broadcasted_iota(jnp.int32, (owned * ROWS, width), 0)
    across = lax.broadcasted_iota(jnp.int32, (owned * ROWS, width), 1)
    hit = down == place * ROWS + lax.rem(across, ROWS)
    landing = jnp.where(hit, 1.0, 0.0).astype(BF16)

    ob_copy.wait_recv()
    for m in range(obl):
        tot = own[m] + oc_recv[m]
        ocn_v[:, m * blk : (m + 1) * blk] = tot[:nflux] / jnp.maximum(tot[nflux : nflux + 1], 1.0)
    ocn_copy = pltpu.make_async_copy(ocn_v, ocn_out, out_sem.at[1])
    ocn_copy.start()

    for c in range(nsub):
        for i in range(owners):
            desc = recv_desc(sums_send.at[i], sums_recv.at[c, i], sum_ssem.at[i, 0], sum_rsem.at[c, i])
            if i == zero_i:
                @pl.when(core != c)
                def _(desc=desc):
                    desc.wait_recv()
            else:
                desc.wait_recv()
    arrived = sums_recv[0] + sums_recv[1]
    arrived = arrived.reshape(width, blk)
    high, low = split(arrived)
    final = jnp.dot(landing, high, preferred_element_type=F32) + jnp.dot(
        landing, low, preferred_element_type=F32
    )
    for a in range(owned):
        tot = final[a * ROWS : (a + 1) * ROWS]
        atm_v[:, a * blk : (a + 1) * blk] = tot[:nflux] / jnp.maximum(tot[nflux : nflux + 1], 1.0)
    atm_copy = pltpu.make_async_copy(atm_v, atm_out, out_sem.at[2])
    atm_copy.start()

    for k in range(half):
        if k == zero_i % half:
            @pl.when(core != zero_core)
            def _(k=k):
                pushes[k].wait_send()
        else:
            pushes[k].wait_send()
    for k in range(half):
        for c in range(nsub):
            copy = row_copies[k * nsub + c]
            if k == zero_i % half:
                @pl.when(jnp.logical_not(jnp.logical_and(core == zero_core, core == c)))
                def _(copy=copy):
                    copy.wait_send()
            else:
                copy.wait_send()
    oc_copy.wait_send()
    pick_copy.wait_send()
    for copy in sum_copies.values():
        copy.wait_send()
    self_copy.wait_send()
    ob_copy.wait_send()
    ocn_copy.wait()
    atm_copy.wait()


def solution(mesh):
    ntile, nsub = mesh.shape["tile"], mesh.shape["sub"]

    def per_device(
        atm_state, ocn_state, need_atm, xb_need, xb_ocn, xb_count, sea_mask, cell_area, w_atm, w_ocn
    ):
        nb, blk, _ = w_atm.shape
        nflux = 4
        mine = need_atm.shape[0]
        half = mine // PAIR
        owners = half * nsub
        entries = mine * nsub
        fields_a, acells = atm_state.shape
        fields_o, ocells = ocn_state.shape
        obl = ocells // blk
        owned = acells // blk
        cells = nb * blk
        dma = pltpu.SemaphoreType.DMA
        return pl.pallas_call(
            functools.partial(kernel, ntile, nsub, blk),
            out_shape=(
                jax.ShapeDtypeStruct((nflux, acells), F32),
                jax.ShapeDtypeStruct((nflux, ocells), F32),
            ),
            in_specs=[pl.BlockSpec(memory_space=pl.ANY)] * 10,
            out_specs=(pl.BlockSpec(memory_space=pl.ANY),) * 2,
            scratch_shapes=[
                pltpu.VMEM((owned, fields_a, blk), BF16),
                pltpu.VMEM((nsub, obl, fields_o, blk), BF16),
                pltpu.SMEM((mine,), jnp.int32),
                pltpu.SMEM((nb,), jnp.int32),
                pltpu.SMEM((nb,), jnp.int32),
                pltpu.SMEM((1,), jnp.int32),
                pltpu.VMEM((1, cells), jnp.int32),
                pltpu.VMEM((1, cells), F32),
                pltpu.VMEM((nb, blk, blk), BF16),
                pltpu.VMEM((nb, blk, blk), BF16),
                pltpu.VMEM((half, owned, fields_a, blk), BF16),
                pltpu.VMEM((entries, fields_a, blk), BF16),
                pltpu.VMEM((half, 1, blk), jnp.int32),
                pltpu.VMEM((owners, 1, blk), jnp.int32),
                pltpu.VMEM((owners, PAIR * ROWS, blk), F32),
                pltpu.VMEM((nsub, owners, PAIR * ROWS, blk), F32),
                pltpu.VMEM((obl, ROWS, blk), F32),
                pltpu.VMEM((obl, ROWS, blk), F32),
                pltpu.VMEM((nflux, acells), F32),
                pltpu.VMEM((nflux, ocells), F32),
                dma((8,)),
                dma((owned + obl,)),
                dma((half,)),
                dma((half,)),
                dma((half * nsub,)),
                dma((owners,)),
                dma(()),
                dma(()),
                dma(()),
                dma(()),
                dma((owners, nsub)),
                dma((nsub, owners)),
                dma(()),
                dma(()),
                dma((3,)),
            ],
            compiler_params=pltpu.CompilerParams(collective_id=0, has_side_effects=True),
        )(
            atm_state, ocn_state, need_atm, xb_need, xb_ocn, xb_count,
            sea_mask.reshape(1, cells), cell_area.reshape(1, cells), w_atm, w_ocn,
        )

    spread_all = P(("tile", "sub"))
    weights = P(("tile", "sub"), None, None)
    return jax.shard_map(
        per_device,
        mesh=mesh,
        in_specs=(
            P(None, ("member", "tile")),
            P(None, ("member", "tile", "sub")),
            spread_all, spread_all, spread_all, spread_all, spread_all, spread_all,
            weights, weights,
        ),
        out_specs=(P(None, ("member", "tile")), P(None, ("member", "tile", "sub"))),
        check_vma=False,
    )
```

time: 72.9 us -> 21.4 us (0.29)
  Pallas kernels: 0 us -> 17.9 us
  starting transfers between devices: 16.6 us -> 0 us
  between operations: 15.6 us -> 1.3 us
  waiting for transfers between devices: 13.3 us -> 0 us
  local copies, waits for them, and re-layouts: 9.76 us -> 1.99 us
  other arithmetic: 7.32 us -> 0 us
  blocking collectives: 7.24 us -> 0 us
  matrix products: 2.39 us -> 0 us
    pallas_call x0 -> x1, Pallas kernels: none -> 17.9 us  [per_device(): pl.pallas_call(functools.partial(kernel, ntile, nsub, blk), out_shape=(ja...]
    all_to_all x3 -> x0, starting transfers between devices: 16.6 us -> none  [the longest x1 7.13 us: per_device(): lax.all_to_all(asked_all, 'tile', split_axis=0, concat_axis=0, tiled=True)]
    all_to_all x3 -> x0, waiting for transfers between devices: 12.3 us -> none  [the longest x1 6.6 us: per_device(): lax.all_to_all(picked.reshape(ntile, depth, fields_a, blk), 'tile', split...]
    psum x1 -> x0, blocking collectives: 3.48 us -> none  [per_device(): totals = lax.psum(owned, 'sub')]
    dot_general x7 -> x0, matrix products: 2.39 us -> none  [the longest x1 0.89 us: per_device(): jnp.einsum('bn,bgj->ngj', select_o, ocn_cells, precision=highest)]
    gather x4 -> x0, local copies, waits for them, and re-layouts: 2.29 us -> none  [the longest x1 0.58 us: per_device(): ocean_table[xb_ocn]]
    unnamed x19 -> x4, local copies, waits for them, and re-layouts: 4.23 us -> 1.99 us
    select_n x4 -> x0, other arithmetic: 2.03 us -> none  [the longest x1 0.7 us: per_device(): jnp.where((flat >= 0)[:, None, None], picked, jnp.zeros_like(picked))]
  transfers between devices with their start and end apart: 4 -> 0, of which waited for: 3 -> 0; matrix products, arithmetic and copies ran while one was open for 9% -> 0% of each run, Pallas kernels for 0% -> 0%
where the time goes in v1:
time: 21.4 us; the launch traced here: 21.2 us
  Pallas kernels  17.9 us (84%)
  local copies, waits for them, and re-layouts  1.99 us (9%)
  between operations  1.3 us (6%)
    pallas_call x1, Pallas kernels, per_device(): pl.pallas_call(functools.partial(kernel, ntile, nsub, blk), out_shape=(ja...  17.9 us
    unnamed x4, local copies, waits for them, and re-layouts  1.99 us

profile of v1, /device:TPU:0, one launch (start us, length us, event | category | flops | bytes accessed | tf_op | source)
XLA Modules:
  0.0 21.2 jit_solution(17552935830293145395)
XLA Ops:
  1.3 17.9 %shard_map.113 = (f32[4,2048]{1,0:T(4,128)}, f32[4,1024]{1,0:T(4,128)}) custom-call(bf16[8,2048]{1,0:T(8,128)(2,1)} %state_hbm.1, bf16[4,1024]{1,0:T(4,128)(2,1)} %ocean_hbm.1, s32[8]{0:T(128)} %need_hbm.1, s32[8]{0:T(128)} %xbn_hbm.1, s32[8]{0:T(128)} %xbo_hbm.1, s32[1]{0:T(128)S(6)} %copy.14.count_hbm, s32[1,1024]{1,0:T(1,128)} %bitcast.2, ...), custom_call_target="tpu_custom_call" | custom-call | tf_op jit(solution)/shard_map/pallas_call | solution.py:401
  19.2 0.0 copy-start
  19.2 1.4 %copy.15 = f32[4,2048]{1,0:T(4,128)} copy(f32[4,2048]{1,0:T(4,128)} %get-tuple-element.4) | data formatting | bytes 65536
  20.6 0.0 copy-done
  20.6 0.6 %copy.16 = f32[4,1024]{1,0:T(4,128)} copy(f32[4,1024]{1,0:T(4,128)S(1)} %copy-done) | data formatting | bytes 32768
Async XLA Ops:
  19.2 1.4 %copy-start = (f32[4,1024]{1,0:T(4,128)S(1)}, f32[4,1024]{1,0:T(4,128)}, u32[]{:S(2)}) copy-start(f32[4,1024]{1,0:T(4,128)} %get-tuple-element.5) | copy-start | bytes 49156

commit v2 on v1

--- a/solution.py
+++ b/solution.py
@@ -26,9 +26,9 @@
     state_hbm, ocean_hbm, need_hbm, xbn_hbm, xbo_hbm, count_hbm, sea_hbm, area_hbm, wa_hbm, wo_hbm,
     atm_out, ocn_out,
     state, octab, need, xbn, xbo, count, sea, area, wa, wo,
-    table, picked, rows_send, rows_recv, sums_send, sums_recv, oc_send, oc_recv, atm_v, ocn_v,
+    table, picked, rows_send, rows_recv, area_send, area_recv, sums_send, sums_recv, oc_send, oc_recv,
     load_sem, block_sem, push_ssem, push_rsem, row_ssem, row_rsem, oc_ssem, oc_rsem,
-    pick_ssem, pick_rsem, sum_ssem, sum_rsem, ob_ssem, ob_rsem, out_sem,
+    pick_ssem, pick_rsem, area_ssem, area_rsem, sum_ssem, sum_rsem, ob_ssem, ob_rsem, keep_sem,
 ):
     me = lax.axis_index("tile")
     core = lax.axis_index("sub")
@@ -40,7 +40,8 @@
     entries = mine * nsub
     owned = state.shape[0]
     obl = octab.shape[1]
-    nflux = atm_v.shape[0]
+    nflux = atm_out.shape[0]
+    flux_lanes = owners * PAIR * nflux
 
     def offset(i):
         return ntile // 2 if i == owners - 1 else i - owners // 2 + 1
@@ -91,7 +92,7 @@
 
     local[0].wait()
     lane = lax.broadcasted_iota(jnp.int32, (1, blk), 1)
-    odd = lax.rem(lane // ROWS, PAIR)
+    odd = jnp.where(lane < flux_lanes, lax.rem(lane // nflux, PAIR), lax.rem(lane, PAIR))
     for k in range(half):
         first = lax.rem(need[PAIR * k], owned)
         second = lax.rem(need[PAIR * k + 1], owned)
@@ -118,7 +119,7 @@
         )
         for k in range(half)
     ]
-    keep = pltpu.make_async_copy(state, table.at[zero_i % half], out_sem.at[0])
+    keep = pltpu.make_async_copy(state, table.at[zero_i % half], keep_sem)
     zero_core = zero_i // half
     order = sorted(range(half), key=lambda k: -abs(offset(k)))
     for k in order:
@@ -197,6 +198,42 @@
     weighted = jnp.where(cell < count[0] * blk, area[...], 0.0)
     wet = weighted * sea[...].astype(F32)
 
+    def spread(both, w, index, number, step, shift):
+        totals = [None] * number
+        for b in range(nb):
+            prod = jnp.dot(both[:, b * blk : (b + 1) * blk], w[b], preferred_element_type=F32)
+            prod = prod[:ROWS] + prod[ROWS:]
+            at = index[b] - shift
+            for n in range(number):
+                term = jnp.where(at == n * step, prod, 0.0)
+                totals[n] = term if totals[n] is None else totals[n] + term
+        return totals
+
+    def send_owners(src, dst, ssem, rsem):
+        copies = []
+        for i in sorted(range(owners), key=lambda i: -abs(offset(i))):
+            for c in range(nsub):
+                if i == zero_i and c > 0:
+                    continue
+                copy = pltpu.make_async_remote_copy(
+                    src_ref=src.at[i],
+                    dst_ref=dst.at[core, i],
+                    send_sem=ssem.at[i, c],
+                    recv_sem=rsem.at[core, i],
+                    device_id={"tile": tile_at(offset(i)), "sub": other if i == zero_i else c},
+                    device_id_type=MESH,
+                )
+                copy.start()
+                copies.append(copy)
+        return copies
+
+    row_id = lax.broadcasted_iota(jnp.int32, (ROWS, blk), 0)
+    areas = jnp.concatenate(split(jnp.broadcast_to(weighted, (ROWS, nb * blk))), axis=0)
+    totals = spread(areas, wa, xbn, owners, PAIR, lax.rem(row_id, PAIR))
+    for i in range(owners):
+        area_send[i] = totals[i][:PAIR]
+    area_recv[core, zero_i] = totals[zero_i][:PAIR]
+
     for k in range(half):
         if k == zero_i % half:
             @pl.when(core == zero_core)
@@ -220,6 +257,7 @@
         device_id_type=MESH,
     )
     pick_copy.start()
+    area_copies = send_owners(area_send, area_recv, area_ssem, area_rsem)
     pick_copy.wait_recv()
     ax = jnp.concatenate(
         [
@@ -240,53 +278,19 @@
     taux = cd * du
     tauy = cd * dv
     pad = jnp.zeros((ROWS - 5, nb * blk), F32)
-    atm_terms = jnp.concatenate([sens * wet, lat * wet, taux * wet, tauy * wet, weighted, pad], 0)
-    both = jnp.concatenate(split(atm_terms), axis=0)
-
-    def spread(both, w, index, number):
-        totals = [None] * number
-        for b in range(nb):
-            prod = jnp.dot(both[:, b * blk : (b + 1) * blk], w[b], preferred_element_type=F32)
-            prod = prod[:ROWS] + prod[ROWS:]
-            at = jnp.full((ROWS, blk), index[b], jnp.int32)
-            for n in range(number):
-                term = jnp.where(at == n, prod, 0.0)
-                totals[n] = term if totals[n] is None else totals[n] + term
-        return totals
-
-    totals = spread(both, wa, xbn, entries)
-    for n in range(entries):
-        sums_send[n // PAIR, (n % PAIR) * ROWS : (n % PAIR + 1) * ROWS] = totals[n]
-    sum_copies = {}
-    for i in sorted(range(owners), key=lambda i: -abs(offset(i))):
-        for c in range(nsub):
-            if i == zero_i:
-                continue
-            sum_copies[i, c] = pltpu.make_async_remote_copy(
-                src_ref=sums_send.at[i],
-                dst_ref=sums_recv.at[core, i],
-                send_sem=sum_ssem.at[i, c],
-                recv_sem=sum_rsem.at[core, i],
-                device_id={"tile": tile_at(offset(i)), "sub": c},
-                device_id_type=MESH,
-            )
-            sum_copies[i, c].start()
-    self_copy = pltpu.make_async_remote_copy(
-        src_ref=sums_send.at[zero_i],
-        dst_ref=sums_recv.at[core, zero_i],
-        send_sem=sum_ssem.at[zero_i, 0],
-        recv_sem=sum_rsem.at[core, zero_i],
-        device_id={"tile": me, "sub": other},
-        device_id_type=MESH,
-    )
-    self_copy.start()
-    for e in range(PAIR):
-        sums_recv[core, zero_i, e * ROWS : (e + 1) * ROWS] = totals[PAIR * zero_i + e]
+    fluxes = [sens * wet, lat * wet, taux * wet, tauy * wet]
+    both = jnp.concatenate(split(jnp.concatenate(fluxes * PAIR, axis=0)), axis=0)
+    totals = spread(both, wa, xbn, owners, PAIR, row_id // nflux)
+    for i in range(owners):
+        sums_send[i] = totals[i]
+    sum_copies = send_owners(sums_send, sums_recv, sum_ssem, sum_rsem)
+    sums_recv[core, zero_i] = totals[zero_i]
 
     heat = (1.0 - albedo) * sw + lw - 0.2 * sst - sens - lat
     fresh = pr - 0.5 * lat
+    pad = jnp.zeros((ROWS - nflux - 1, nb * blk), F32)
     ocn_terms = jnp.concatenate([heat * wet, taux * wet, tauy * wet, fresh * wet, wet, pad], 0)
-    ototals = spread(jnp.concatenate(split(ocn_terms), axis=0), wo, xbo, obl * nsub)
+    ototals = spread(jnp.concatenate(split(ocn_terms), axis=0), wo, xbo, obl * nsub, 1, 0)
     own = []
     for m in range(obl):
         low, high = ototals[m], ototals[obl + m]
@@ -316,43 +320,54 @@
                 desc.wait_recv()
         else:
             desc.wait_recv()
-    width = owners * PAIR * ROWS
     places = jnp.concatenate([rows_recv[i] for i in range(owners)], axis=0)
-    slot_of = lax.broadcasted_iota(jnp.int32, (owners, width), 1) // (PAIR * ROWS)
-    mask = slot_of == lax.broadcasted_iota(jnp.int32, (owners, width), 0)
+    lanes = lax.broadcasted_iota(jnp.int32, (owners, blk), 1)
+    slot_of = jnp.where(
+        lanes < flux_lanes, lanes // (PAIR * nflux), (lanes - flux_lanes) // PAIR
+    )
+    mask = slot_of == lax.broadcasted_iota(jnp.int32, (owners, blk), 0)
     place = jnp.sum(jnp.where(mask, places, 0), axis=0, keepdims=True)
-    down = lax.broadcasted_iota(jnp.int32, (owned * ROWS, width), 0)
-    across = lax.broadcasted_iota(jnp.int32, (owned * ROWS, width), 1)
-    hit = down == place * ROWS + lax.rem(across, ROWS)
-    landing = jnp.where(hit, 1.0, 0.0).astype(BF16)
+    down = lax.broadcasted_iota(jnp.int32, (owned * nflux, blk), 0)
+    across = lax.broadcasted_iota(jnp.int32, (owned * nflux, blk), 1)
+    hit = jnp.logical_and(
+        down // nflux == place,
+        jnp.logical_or(across >= flux_lanes, lax.rem(down, nflux) == lax.rem(across, nflux)),
+    )
+    landing = jnp.where(hit, 1.0, 0.0)
+    landing_flux = landing[:, :flux_lanes].astype(BF16)
+    landing_area = landing[:, flux_lanes : flux_lanes + owners * PAIR].astype(BF16)
+
+    def land(landing, value):
+        high, low = split(value)
+        return jnp.dot(landing, high, preferred_element_type=F32) + jnp.dot(
+            landing, low, preferred_element_type=F32
+        )
+
+    def wait_owners(src, dst, ssem, rsem):
+        for c in range(nsub):
+            for i in range(owners):
+                desc = recv_desc(src.at[i], dst.at[c, i], ssem.at[i, 0], rsem.at[c, i])
+                if i == zero_i:
+                    @pl.when(core != c)
+                    def _(desc=desc):
+                        desc.wait_recv()
+                else:
+                    desc.wait_recv()
 
     ob_copy.wait_recv()
     for m in range(obl):
         tot = own[m] + oc_recv[m]
-        ocn_v[:, m * blk : (m + 1) * blk] = tot[:nflux] / jnp.maximum(tot[nflux : nflux + 1], 1.0)
-    ocn_copy = pltpu.make_async_copy(ocn_v, ocn_out, out_sem.at[1])
-    ocn_copy.start()
-
-    for c in range(nsub):
-        for i in range(owners):
-            desc = recv_desc(sums_send.at[i], sums_recv.at[c, i], sum_ssem.at[i, 0], sum_rsem.at[c, i])
-            if i == zero_i:
-                @pl.when(core != c)
-                def _(desc=desc):
-                    desc.wait_recv()
-            else:
-                desc.wait_recv()
-    arrived = sums_recv[0] + sums_recv[1]
-    arrived = arrived.reshape(width, blk)
-    high, low = split(arrived)
-    final = jnp.dot(landing, high, preferred_element_type=F32) + jnp.dot(
-        landing, low, preferred_element_type=F32
-    )
+        ocn_out[:, m * blk : (m + 1) * blk] = tot[:nflux] / jnp.maximum(tot[nflux : nflux + 1], 1.0)
+
+    wait_owners(area_send, area_recv, area_ssem, area_rsem)
+    arrived = jnp.concatenate([area_recv[0, i] + area_recv[1, i] for i in range(owners)], axis=0)
+    scale = 1.0 / jnp.maximum(land(landing_area, arrived), 1.0)
+
+    wait_owners(sums_send, sums_recv, sum_ssem, sum_rsem)
+    arrived = (sums_recv[0] + sums_recv[1]).reshape(flux_lanes, blk)
+    final = land(landing_flux, arrived) * scale
     for a in range(owned):
-        tot = final[a * ROWS : (a + 1) * ROWS]
-        atm_v[:, a * blk : (a + 1) * blk] = tot[:nflux] / jnp.maximum(tot[nflux : nflux + 1], 1.0)
-    atm_copy = pltpu.make_async_copy(atm_v, atm_out, out_sem.at[2])
-    atm_copy.start()
+        atm_out[:, a * blk : (a + 1) * blk] = final[a * nflux : (a + 1) * nflux]
 
     for k in range(half):
         if k == zero_i % half:
@@ -372,12 +387,9 @@
                 copy.wait_send()
     oc_copy.wait_send()
     pick_copy.wait_send()
-    for copy in sum_copies.values():
+    for copy in area_copies + sum_copies:
         copy.wait_send()
-    self_copy.wait_send()
     ob_copy.wait_send()
-    ocn_copy.wait()
-    atm_copy.wait()
 
 
 def solution(mesh):
@@ -401,11 +413,11 @@
         return pl.pallas_call(
             functools.partial(kernel, ntile, nsub, blk),
             out_shape=(
-                jax.ShapeDtypeStruct((nflux, acells), F32),
-                jax.ShapeDtypeStruct((nflux, ocells), F32),
+                pltpu.VMEM((nflux, acells), F32),
+                pltpu.VMEM((nflux, ocells), F32),
             ),
-            in_specs=[pl.BlockSpec(memory_space=pl.ANY)] * 10,
-            out_specs=(pl.BlockSpec(memory_space=pl.ANY),) * 2,
+            in_specs=[pl.BlockSpec(memory_space=pltpu.HBM)] * 10,
+            out_specs=(pl.BlockSpec(memory_space=pltpu.VMEM),) * 2,
             scratch_shapes=[
                 pltpu.VMEM((owned, fields_a, blk), BF16),
                 pltpu.VMEM((nsub, obl, fields_o, blk), BF16),
@@ -421,12 +433,12 @@
                 pltpu.VMEM((entries, fields_a, blk), BF16),
                 pltpu.VMEM((half, 1, blk), jnp.int32),
                 pltpu.VMEM((owners, 1, blk), jnp.int32),
-                pltpu.VMEM((owners, PAIR * ROWS, blk), F32),
-                pltpu.VMEM((nsub, owners, PAIR * ROWS, blk), F32),
+                pltpu.VMEM((owners, PAIR, blk), F32),
+                pltpu.VMEM((nsub, owners, PAIR, blk), F32),
+                pltpu.VMEM((owners, PAIR * nflux, blk), F32),
+                pltpu.VMEM((nsub, owners, PAIR * nflux, blk), F32),
                 pltpu.VMEM((obl, ROWS, blk), F32),
                 pltpu.VMEM((obl, ROWS, blk), F32),
-                pltpu.VMEM((nflux, acells), F32),
-                pltpu.VMEM((nflux, ocells), F32),
                 dma((8,)),
                 dma((owned + obl,)),
                 dma((half,)),
@@ -439,9 +451,11 @@
                 dma(()),
                 dma((owners, nsub)),
                 dma((nsub, owners)),
-                dma(()),
-                dma(()),
-                dma((3,)),
+                dma((owners, nsub)),
+                dma((nsub, owners)),
+                dma(()),
+                dma(()),
+                dma(()),
             ],
             compiler_params=pltpu.CompilerParams(collective_id=0, has_side_effects=True),
         )(

time: 21.4 us -> 19.4 us (0.907)
  Pallas kernels: 17.9 us -> 16.7 us
  local copies, waits for them, and re-layouts: 1.99 us -> 1.22 us
    pallas_call x1, Pallas kernels: 17.9 us -> 16.7 us  [per_device(): pl.pallas_call(functools.partial(kernel, ntile, nsub, blk), out_shape=(pl...]
    unnamed x4 -> x2, local copies, waits for them, and re-layouts: 1.99 us -> 1.22 us
where the time goes in v2:
time: 19.4 us; the launch traced here: 19.3 us
  Pallas kernels  16.7 us (86%)
  between operations  1.29 us (7%)
  local copies, waits for them, and re-layouts  1.22 us (6%)
    pallas_call x1, Pallas kernels, per_device(): pl.pallas_call(functools.partial(kernel, ntile, nsub, blk), out_shape=(pl...  16.7 us
    unnamed x2, local copies, waits for them, and re-layouts  1.22 us

profile of v2, /device:TPU:0, one launch (start us, length us, event | category | flops | bytes accessed | tf_op | source)
XLA Modules:
  0.0 19.3 jit_solution(1424571663822865301)
XLA Ops:
  1.3 16.7 %shard_map.113 = (f32[4,2048]{1,0:T(4,128)S(1)}, f32[4,1024]{1,0:T(4,128)S(1)}) custom-call(bf16[8,2048]{1,0:T(8,128)(2,1)} %state_hbm.1, bf16[4,1024]{1,0:T(4,128)(2,1)} %ocean_hbm.1, s32[8]{0:T(128)} %need_hbm.1, s32[8]{0:T(128)} %xbn_hbm.1, s32[8]{0:T(128)} %xbo_hbm.1, s32[1]{0:T(128)S(6)} %copy.16.count_hbm, s32[1,1024]{1,0:T(1,128)} %bitcast.2, ...), custom_call_target="tpu_custom_call" | custom-call | tf_op jit(solution)/shard_map/pallas_call | solution.py:413
  18.0 0.6 %copy.14 = f32[4,2048]{1,0:T(4,128)} copy(f32[4,2048]{1,0:T(4,128)S(1)} %get-tuple-element.2) | data formatting | bytes 65536
  18.6 0.6 %copy.15 = f32[4,1024]{1,0:T(4,128)} copy(f32[4,1024]{1,0:T(4,128)S(1)} %get-tuple-element.3) | data formatting | bytes 32768

commit v3 on v2

--- a/solution.py
+++ b/solution.py
@@ -392,6 +392,17 @@
     ob_copy.wait_send()
 
 
+def write_out(atm, ocn, atm_hbm, ocn_hbm, sem):
+    copies = [
+        pltpu.make_async_copy(src, dst, sem.at[k])
+        for k, (src, dst) in enumerate([(atm, atm_hbm), (ocn, ocn_hbm)])
+    ]
+    for copy in copies:
+        copy.start()
+    for copy in copies:
+        copy.wait()
+
+
 def solution(mesh):
     ntile, nsub = mesh.shape["tile"], mesh.shape["sub"]
 
@@ -410,7 +421,7 @@
         owned = acells // blk
         cells = nb * blk
         dma = pltpu.SemaphoreType.DMA
-        return pl.pallas_call(
+        fluxes = pl.pallas_call(
             functools.partial(kernel, ntile, nsub, blk),
             out_shape=(
                 pltpu.VMEM((nflux, acells), F32),
@@ -462,6 +473,14 @@
             atm_state, ocn_state, need_atm, xb_need, xb_ocn, xb_count,
             sea_mask.reshape(1, cells), cell_area.reshape(1, cells), w_atm, w_ocn,
         )
+        return pl.pallas_call(
+            write_out,
+            out_shape=tuple(jax.ShapeDtypeStruct(f.shape, F32) for f in fluxes),
+            in_specs=[pl.BlockSpec(memory_space=pltpu.VMEM)] * 2,
+            out_specs=(pl.BlockSpec(memory_space=pltpu.HBM),) * 2,
+            scratch_shapes=[dma((2,))],
+            compiler_params=pltpu.CompilerParams(vmem_limit_bytes=2**20),
+        )(*fluxes)
 
     spread_all = P(("tile", "sub"))
     weights = P(("tile", "sub"), None, None)

time: 19.4 us -> 18.8 us (0.969)
  local copies, waits for them, and re-layouts: 1.22 us -> 0 us
  Pallas kernels: 16.7 us -> 17.4 us
    unnamed x2 -> x0, local copies, waits for them, and re-layouts: 1.22 us -> none
    pallas_call x0 -> x1, Pallas kernels: none -> 0.64 us  [per_device(): pl.pallas_call(write_out, out_shape=tuple((jax.ShapeDtypeStruct(f.shape,...]
where the time goes in v3:
time: 18.8 us; the launch traced here: 18.7 us
  Pallas kernels  17.4 us (93%)
  between operations  1.29 us (7%)
    pallas_call x1, Pallas kernels, per_device(): pl.pallas_call(functools.partial(kernel, ntile, nsub, blk), out_shape=(pl...  16.7 us
    pallas_call x1, Pallas kernels, per_device(): pl.pallas_call(write_out, out_shape=tuple((jax.ShapeDtypeStruct(f.shape,...  0.64 us

profile of v3, /device:TPU:0, one launch (start us, length us, event | category | flops | bytes accessed | tf_op | source)
XLA Modules:
  0.0 18.7 jit_solution(4428569337004357483)
XLA Ops:
  1.3 16.7 %shard_map.113 = (f32[4,2048]{1,0:T(4,128)S(1)}, f32[4,1024]{1,0:T(4,128)S(1)}) custom-call(bf16[8,2048]{1,0:T(8,128)(2,1)} %state_hbm.1, bf16[4,1024]{1,0:T(4,128)(2,1)} %ocean_hbm.1, s32[8]{0:T(128)} %need_hbm.1, s32[8]{0:T(128)} %xbn_hbm.1, s32[8]{0:T(128)} %xbo_hbm.1, s32[1]{0:T(128)S(6)} %copy.12.count_hbm, s32[1,1024]{1,0:T(1,128)} %bitcast.2, ...), custom_call_target="tpu_custom_call" | custom-call | tf_op jit(solution)/shard_map/pallas_call | solution.py:424
  18.0 0.6 %shard_map.114 = (f32[4,2048]{1,0:T(4,128)}, f32[4,1024]{1,0:T(4,128)}) custom-call(f32[4,2048]{1,0:T(4,128)S(1)} %get-tuple-element.4.atm, f32[4,1024]{1,0:T(4,128)S(1)} %get-tuple-element.5.ocn), custom_call_target="tpu_custom_call" | custom-call | tf_op jit(solution)/shard_map/pallas_call | solution.py:476

commit v4 on v3

--- a/solution.py
+++ b/solution.py
@@ -102,37 +102,45 @@
     pl.semaphore_wait(barrier, owners * nsub - 1)
 
     def delta_of(k):
-        out = jnp.int32(0)
-        for c in range(nsub):
-            out = jnp.where(core == c, jnp.int32(offset(c * half + k)), out)
-        return out
+        i = core * half + k
+        return jnp.where(i == owners - 1, ntile // 2, i - owners // 2 + 1)
 
     deltas = [delta_of(k) for k in range(half)]
-    pushes = [
-        pltpu.make_async_remote_copy(
+
+    def push_of(k, delta):
+        return pltpu.make_async_remote_copy(
             src_ref=state,
             dst_ref=table.at[k],
             send_sem=push_ssem.at[k],
             recv_sem=push_rsem.at[k],
-            device_id={"tile": tile_at(-deltas[k]), "sub": core},
+            device_id={"tile": tile_at(-delta), "sub": core},
             device_id_type=MESH,
         )
-        for k in range(half)
-    ]
+
+    pushes = [push_of(k, deltas[k]) for k in range(half)]
     keep = pltpu.make_async_copy(state, table.at[zero_i % half], keep_sem)
     zero_core = zero_i // half
-    order = sorted(range(half), key=lambda k: -abs(offset(k)))
-    for k in order:
-        if k == zero_i % half:
+    far = [jnp.abs(tile_at(-delta) - me) for delta in deltas]
+    for rank in range(half):
+        pick = jnp.int32(0)
+        for k in range(half):
+            ahead = jnp.int32(0)
+            for o in range(half):
+                if o != k:
+                    first = far[o] >= far[k] if o < k else far[o] > far[k]
+                    ahead = ahead + jnp.where(first, 1, 0)
+            pick = pick + jnp.where(ahead == rank, k, 0)
+        push = push_of(pick, delta_of(pick))
+        if rank == half - 1:
             @pl.when(core == zero_core)
             def _():
                 keep.start()
 
             @pl.when(core != zero_core)
-            def _(k=k):
-                pushes[k].start()
+            def _(push=push):
+                push.start()
         else:
-            pushes[k].start()
+            push.start()
     oc_copy = pltpu.make_async_remote_copy(
         src_ref=octab.at[core],
         dst_ref=octab.at[core],

time: 18.8 us -> 18.8 us (level)
  no operation moved by 1% of the time
where the time goes in v4:
time: 18.8 us; the launch traced here: 18.7 us
  Pallas kernels  17.4 us (93%)
  between operations  1.29 us (7%)
    pallas_call x1, Pallas kernels, per_device(): pl.pallas_call(functools.partial(kernel, ntile, nsub, blk), out_shape=(pl...  16.7 us
    pallas_call x1, Pallas kernels, per_device(): pl.pallas_call(write_out, out_shape=tuple((jax.ShapeDtypeStruct(f.shape,...  0.64 us

profile of v4, /device:TPU:0, one launch (start us, length us, event | category | flops | bytes accessed | tf_op | source)
XLA Modules:
  0.0 18.7 jit_solution(10692590167786329764)
XLA Ops:
  1.3 16.7 %shard_map.113 = (f32[4,2048]{1,0:T(4,128)S(1)}, f32[4,1024]{1,0:T(4,128)S(1)}) custom-call(bf16[8,2048]{1,0:T(8,128)(2,1)} %state_hbm.1, bf16[4,1024]{1,0:T(4,128)(2,1)} %ocean_hbm.1, s32[8]{0:T(128)} %need_hbm.1, s32[8]{0:T(128)} %xbn_hbm.1, s32[8]{0:T(128)} %xbo_hbm.1, s32[1]{0:T(128)S(6)} %copy.12.count_hbm, s32[1,1024]{1,0:T(1,128)} %bitcast.2, ...), custom_call_target="tpu_custom_call" | custom-call | tf_op jit(solution)/shard_map/pallas_call | solution.py:432
  18.0 0.6 %shard_map.114 = (f32[4,2048]{1,0:T(4,128)}, f32[4,1024]{1,0:T(4,128)}) custom-call(f32[4,2048]{1,0:T(4,128)S(1)} %get-tuple-element.4.atm, f32[4,1024]{1,0:T(4,128)S(1)} %get-tuple-element.5.ocn), custom_call_target="tpu_custom_call" | custom-call | tf_op jit(solution)/shard_map/pallas_call | solution.py:484

commit v5 on v4

--- a/solution.py
+++ b/solution.py
@@ -51,6 +51,16 @@
 
     zero_i = [i for i in range(owners) if offset(i) == 0][0]
 
+    barrier = pltpu.get_barrier_semaphore()
+    for i in sorted(range(owners), key=lambda i: -abs(offset(i))):
+        for c in range(nsub):
+            if i == zero_i:
+                continue
+            pl.semaphore_signal(
+                barrier, inc=1, device_id={"tile": tile_at(offset(i)), "sub": c}, device_id_type=MESH
+            )
+    pl.semaphore_signal(barrier, inc=1, device_id={"tile": me, "sub": other}, device_id_type=MESH)
+
     local = [
         pltpu.make_async_copy(src, dst, load_sem.at[k])
         for k, (src, dst) in enumerate(
@@ -79,16 +89,6 @@
     ]
     for copy in blocks + local:
         copy.start()
-
-    barrier = pltpu.get_barrier_semaphore()
-    for i in range(owners):
-        for c in range(nsub):
-            if i == zero_i:
-                continue
-            pl.semaphore_signal(
-                barrier, inc=1, device_id={"tile": tile_at(offset(i)), "sub": c}, device_id_type=MESH
-            )
-    pl.semaphore_signal(barrier, inc=1, device_id={"tile": me, "sub": other}, device_id_type=MESH)
 
     local[0].wait()
     lane = lax.broadcasted_iota(jnp.int32, (1, blk), 1)

time: 18.8 us -> 18.8 us (level)
  no operation moved by 1% of the time
where the time goes in v5:
time: 18.8 us; the launch traced here: 18.7 us
  Pallas kernels  17.4 us (93%)
  between operations  1.29 us (7%)
    pallas_call x1, Pallas kernels, per_device(): pl.pallas_call(functools.partial(kernel, ntile, nsub, blk), out_shape=(pl...  16.8 us
    pallas_call x1, Pallas kernels, per_device(): pl.pallas_call(write_out, out_shape=tuple((jax.ShapeDtypeStruct(f.shape,...  0.64 us

profile of v5, /device:TPU:0, one launch (start us, length us, event | category | flops | bytes accessed | tf_op | source)
XLA Modules:
  0.0 18.7 jit_solution(15996118308832590730)
XLA Ops:
  1.3 16.8 %shard_map.113 = (f32[4,2048]{1,0:T(4,128)S(1)}, f32[4,1024]{1,0:T(4,128)S(1)}) custom-call(bf16[8,2048]{1,0:T(8,128)(2,1)} %state_hbm.1, bf16[4,1024]{1,0:T(4,128)(2,1)} %ocean_hbm.1, s32[8]{0:T(128)} %need_hbm.1, s32[8]{0:T(128)} %xbn_hbm.1, s32[8]{0:T(128)} %xbo_hbm.1, s32[1]{0:T(128)S(6)} %copy.12.count_hbm, s32[1,1024]{1,0:T(1,128)} %bitcast.2, ...), custom_call_target="tpu_custom_call" | custom-call | tf_op jit(solution)/shard_map/pallas_call | solution.py:432
  18.0 0.6 %shard_map.114 = (f32[4,2048]{1,0:T(4,128)}, f32[4,1024]{1,0:T(4,128)}) custom-call(f32[4,2048]{1,0:T(4,128)S(1)} %get-tuple-element.4.atm, f32[4,1024]{1,0:T(4,128)S(1)} %get-tuple-element.5.ocn), custom_call_target="tpu_custom_call" | custom-call | tf_op jit(solution)/shard_map/pallas_call | solution.py:484
